TPU v7x, 32 devices: a whole 2x2x4 slice. The times are simulated.
32 devices in a mesh: tm: 8 (over z, x), chan: 4 (over y, core).
Axes of the slice: x: 2, y: 2, z: 4, core: 2. Of those that a mesh axis runs over, the one named last changes fastest.
Arguments:
- surveillance: bfloat16 [128, 1024, 256], P(('chan', 'tm')), parts along dimension 0, may hold values from -6 to 6
- ref_samples: bfloat16 [32, 1040, 256], P('tm'), may hold values from -6 to 6
- block_ids: int32 [32], P('tm'), may hold values from 0 to 31, each once
- walk: int32 [32], P('tm'), may hold values from 0 to 63
- cfar_guard: int32 [2048], P('tm'), may hold values from 1 to 8
- cfar_window: int32 [2048], P('tm'), may hold values from 1 to 16
Outputs:
- detection: float32 [8192, 512], P(('chan', 'tm')), parts along dimension 0
There are 4 independent parts, one for each index of `chan`. A program takes and returns all parts, laid end to end along the dimension named above; an argument that names none is the same for every part. Nothing has to cross between parts.
Inputs may be any that keep to these rules, and one draw needn't show every extreme that they name: block_ids names each of 0 to 31 exactly once.
All inputs are finite; a program needn't handle non-finite values.
Results may differ from a plain program's by a relative error of at most 0.0003.
Values sent between devices are 32-bit elements; how exact they have to be, the bound alone decides.
A program may use at most 64 MiB of HBM per device.

v0:
```python
import functools
import math

import numpy as np
import jax
import jax.numpy as jnp
from jax import lax
from jax.experimental import pallas as pl
from jax.experimental.pallas import tpu as pltpu
from jax.sharding import PartitionSpec as P

D = 2048
DOP = 512
SEGS = 64
GUARD_MAX = 8
WIN_MAX = 16
REACH = GUARD_MAX + WIN_MAX
LANES = 128
SEG_ROWS = D // LANES
CHUNK = SEG_ROWS * SEG_ROWS
MESH = pl.DeviceIdType.MESH
F32 = jnp.float32
BF16 = jnp.bfloat16


def window_rows(span):
    return max(s % LANES + span + 2 * REACH for s in range(0, D, span)) // LANES + 1


def iota(shape, dim):
    return lax.broadcasted_iota(jnp.int32, shape, dim)


def split(x):
    high = x.astype(BF16)
    return high, (x - high.astype(F32)).astype(BF16)


def mm(a, b, dims=((1,), (0,))):
    return lax.dot_general(a, b, (dims, ((), ())), preferred_element_type=F32)


def mm3(a, high, low):
    a_high, a_low = split(a)
    return mm(a_high, high) + (mm(a_low, high) + mm(a_high, low))


def correlate_kernel(
    span, walk_ref, ids_ref, s_ref, e_ref, swap_ref, pick_ref, out_ref,
    lhs_ref, rhs_ref, diag_ref, send, got, send_sem, recv_sem,
):
    block = pl.program_id(0)
    chunks = s_ref.shape[1] // CHUNK
    devices, rows_sent = out_ref.shape[0], out_ref.shape[1]
    blocks = out_ref.shape[2] // 2
    me = lax.axis_index("tm")
    barrier = pltpu.get_barrier_semaphore()
    peers = [lax.rem(me + k, devices) for k in range(1, devices)]

    @pl.when(block == 0)
    def _():
        for peer in peers:
            pl.semaphore_signal(barrier, inc=1, device_id={"tm": peer}, device_id_type=MESH)
        diag_ref[...] = jnp.zeros_like(diag_ref)

    def finish(done):
        x = diag_ref[...].reshape(2 * SEG_ROWS * 8, LANES)
        sub = iota(x.shape, 0)
        for bit in (4, 2, 1):
            x = jnp.where((sub & bit) != 0, pltpu.roll(x, LANES - bit, 1), x)
        high, low = split(x)
        x = mm(pick_ref[...], high) + mm(pick_ref[...], low)
        shift = walk_ref[done] + REACH
        place = iota((LANES, LANES), 0) + iota((LANES, LANES), 1) - shift
        turn = jnp.where((place & (LANES - 1)) == 0, 1.0, 0.0).astype(BF16)
        high = x.astype(BF16)
        mid, low = split(x - high.astype(F32))
        x = mm(high, turn) + (mm(mid, turn) + mm(low, turn))
        lane = iota((SEG_ROWS, LANES), 1)
        label = jnp.full((1, LANES), ids_ref[done], jnp.int32).astype(F32)
        zero = jnp.zeros((1, LANES), F32)
        for part in range(2):
            own = x[part * SEG_ROWS : (part + 1) * SEG_ROWS]
            above = jnp.concatenate([zero, own[: SEG_ROWS - 1]], 0)
            tail = jnp.where(lane[:1] < REACH, own[SEG_ROWS - 1 :], 0.0)
            own = jnp.where(lane < shift, above, own)
            slot = 2 * done + part
            for dev in range(devices):
                first = dev * span // LANES
                for r in range(rows_sent):
                    at = first + r
                    row = own[at : at + 1] if at < SEG_ROWS else tail if at == SEG_ROWS else zero
                    if r == rows_sent - 1:
                        row = jnp.where(lane[:1] == LANES - 1, label, row)
                    send[dev, r, pl.ds(slot, 1), :] = row

    finish(jnp.maximum(block - 1, 0))

    swap = swap_ref[...]
    for ch in range(chunks):
        at = ch * CHUNK
        turned = mm(s_ref[0, at : at + CHUNK, :], swap, ((0,), (0,)))
        lhs_ref[:, at : at + CHUNK] = turned.astype(BF16)
        late = at + SEG_ROWS
        rhs_ref[ch, CHUNK:, :] = mm(swap, e_ref[0, late : late + CHUNK, :]).astype(BF16)
        rhs_ref[ch, :CHUNK, :] = mm(swap, e_ref[0, at : at + CHUNK, :]).astype(BF16)

    def product(a):
        off = (SEG_ROWS - a) * SEG_ROWS
        rhs = jnp.concatenate([rhs_ref[ch, off : off + CHUNK, :] for ch in range(chunks)], 0)
        g = mm(lhs_ref[...], rhs)
        return (
            g[:LANES, :LANES] + g[LANES:, LANES:],
            g[LANES:, :LANES] - g[:LANES, LANES:],
        )

    lower = iota((LANES, LANES), 1) <= iota((LANES, LANES), 0)
    later = product(SEG_ROWS)
    for a in reversed(range(SEG_ROWS)):
        here = product(a)
        for part in range(2):
            x = jnp.where(lower, here[part], later[part])
            half = LANES // 2
            while half >= 8:
                x = x[:half] + pltpu.roll(x[half:], LANES - half, 1)
                half //= 2
            diag_ref[part, a] = x
        later = here

    @pl.when(block == blocks - 1)
    def _():
        finish(block)
        pl.semaphore_wait(barrier, devices - 1)
        copies = []
        for k, peer in enumerate(peers):
            copy = pltpu.make_async_remote_copy(
                src_ref=send.at[peer],
                dst_ref=got.at[me],
                send_sem=send_sem.at[k],
                recv_sem=recv_sem.at[k],
                device_id={"tm": peer},
                device_id_type=MESH,
            )
            copy.start()
            copies.append(copy)
        got[me] = send[me]
        for copy in copies:
            copy.wait()
        out_ref[...] = got[...]


def cosine(count):
    wrapped = ((count + DOP // 2) & (DOP - 1)) - DOP // 2
    z = (DOP // 4 - jnp.abs(wrapped)).astype(F32) * (2.0 * math.pi / DOP)
    z2 = z * z
    poly = -1.0 / 39916800.0
    for c in (1.0 / 362880.0, -1.0 / 5040.0, 1.0 / 120.0, -1.0 / 6.0, 1.0):
        poly = poly * z2 + c
    return z * poly


def map_kernel(
    span, got, guard_ref, size_ref, dft_high, dft_low, tab_high, tab_low, ker_high, ker_low,
    out_ref, power_ref, coef_ref,
):
    me = lax.axis_index("tm")
    devices, rows_sent, per = got.shape[:3]
    total = devices * per // 2
    if span % LANES == 0:
        lead, width = REACH, span + 2 * REACH
    else:
        width = rows_sent * LANES
        lead = pl.multiple_of(lax.rem(me * span, LANES) + REACH, 8)
    guard = guard_ref[...].astype(F32)
    size = size_ref[...].astype(F32)
    guard = jnp.transpose(jnp.broadcast_to(guard, (LANES, span)))
    outer = guard + jnp.transpose(jnp.broadcast_to(size, (LANES, span)))
    dist = iota((span, LANES), 1).astype(F32)
    inside = jnp.where((dist > guard) & (dist <= outer), 1.0, 0.0).astype(BF16)
    kernel = mm(inside, ker_high[...]) + mm(inside, ker_low[...])
    guard, outer = guard[:, :1], outer[:, :1]
    dist = jnp.abs(iota((span, width), 1) - lead - iota((span, width), 0)).astype(F32)
    band = jnp.where((dist > guard) & (dist <= outer), 1.0, 0.0).astype(BF16)
    spot = (me * span + iota((span, 1), 0)).astype(F32)
    last = (D - 1) - spot
    count = jnp.minimum(spot, outer) - jnp.minimum(spot, guard)
    count = count + jnp.minimum(last, outer) - jnp.minimum(last, guard)
    weight = 1.0 / (count + 2.0 * (outer - guard))

    rows = [[got[dev, r] for r in range(rows_sent)] for dev in range(devices)]
    stacked = jnp.concatenate([jnp.concatenate(r, 1) for r in rows], 0)
    ids = stacked[:, rows_sent * LANES - 1 :].astype(jnp.int32)
    shape = (devices * per, DOP)
    turns = ids * iota(shape, 1) - (DOP // 4) * (iota(shape, 0) & 1)
    mix_re_high, mix_re_low = split(cosine(turns))
    mix_im_high, mix_im_low = split(cosine(turns + DOP // 4))
    corr = jnp.transpose(stacked)[:width]
    corr_high, corr_low = split(corr)
    norm = 1.0 / (total * SEGS * D)
    re = mm(corr_high, mix_re_high) + (mm(corr_low, mix_re_high) + mm(corr_high, mix_re_low))
    im = mm(corr_high, mix_im_high) + (mm(corr_low, mix_im_high) + mm(corr_high, mix_im_low))
    power = (re * re + im * im) * norm
    floor = jnp.sum(corr * corr, axis=1, keepdims=True) * norm
    coef = mm3(power, dft_high[...], dft_low[...])
    if span % LANES == 0:
        power_c = power[lead : lead + span]
        coef_c = coef[lead : lead + span]
        floor_c = floor[lead : lead + span]
    else:
        power_ref[:, :DOP] = power
        power_ref[:, DOP:] = jnp.broadcast_to(floor, (width, LANES))
        coef_ref[...] = coef
        power_c = power_ref[pl.ds(lead, span), :DOP]
        floor_c = power_ref[pl.ds(lead, span), DOP:][:, :1]
        coef_c = coef_ref[pl.ds(lead, span), :]
    coef_high, coef_low = split(coef)
    sums = mm(band, coef_high) + mm(band, coef_low) + coef_c * kernel
    noise = mm3(sums, tab_high[...], tab_low[...]) * weight
    out_ref[...] = (power_c - floor_c) / (0.25 + noise)


def np_split(x):
    high = x.astype(BF16)
    return jnp.asarray(high), jnp.asarray((x - high.astype(np.float64)).astype(BF16))


def tables(total):
    lag, freq = np.arange(total), np.arange(DOP)
    angle = 2.0 * np.pi / DOP * ((lag[:, None] * freq[None, :]) % DOP)
    tab = np.concatenate([np.cos(angle), np.sin(angle)], 0)
    scale = np.where(lag == 0, 1.0, 2.0) / DOP
    dft = tab.T * np.concatenate([scale, scale])[None, :]
    dist = np.arange(LANES)
    ker = 2.0 * np.cos(2.0 * np.pi / DOP * ((dist[:, None] * lag[None, :]) % DOP))
    ker = np.concatenate([ker, ker], 1)
    return (*np_split(dft), *np_split(tab), *np_split(ker))


def body(surveillance, ref_samples, block_ids, walk, cfar_guard, cfar_window):
    blocks, rows_all = surveillance.shape[:2]
    devices = lax.axis_size("tm")
    total = blocks * devices
    span = D // devices
    rows_sent = window_rows(span)
    chunks = rows_all // CHUNK
    send_shape = (devices, rows_sent, 2 * blocks, LANES)
    smem = pl.BlockSpec(memory_space=pltpu.SMEM)
    vmem = pl.BlockSpec(memory_space=pltpu.VMEM)
    place = np.arange(CHUNK)
    swap = place[None, :] == (place % SEG_ROWS * SEG_ROWS + place // SEG_ROWS)[:, None]
    pick = np.arange(2 * SEG_ROWS)[:, None] == (np.arange(16 * SEG_ROWS) // 8)[None, :]
    windows = pl.pallas_call(
        functools.partial(correlate_kernel, span),
        grid=(blocks,),
        out_shape=jax.ShapeDtypeStruct(send_shape, F32),
        in_specs=[
            smem,
            smem,
            pl.BlockSpec((1,) + surveillance.shape[1:], lambda j: (j, 0, 0)),
            pl.BlockSpec((1,) + ref_samples.shape[1:], lambda j: (j, 0, 0)),
            vmem,
            vmem,
        ],
        out_specs=vmem,
        scratch_shapes=[
            pltpu.VMEM((2 * LANES, rows_all), BF16),
            pltpu.VMEM((chunks, 2 * CHUNK, 2 * LANES), BF16),
            pltpu.VMEM((2, SEG_ROWS, 8, LANES), F32),
            pltpu.VMEM(send_shape, F32),
            pltpu.VMEM(send_shape, F32),
            pltpu.SemaphoreType.DMA((devices,)),
            pltpu.SemaphoreType.DMA((devices,)),
        ],
        compiler_params=pltpu.CompilerParams(
            dimension_semantics=("arbitrary",), collective_id=0, has_side_effects=True
        ),
        name="correlate",
    )(walk, block_ids, surveillance, ref_samples, jnp.asarray(swap.astype(BF16)), jnp.asarray(pick.astype(BF16)))
    width = span + 2 * REACH if span % LANES == 0 else rows_sent * LANES
    return pl.pallas_call(
        functools.partial(map_kernel, span),
        out_shape=jax.ShapeDtypeStruct((span, DOP), F32),
        in_specs=[vmem] * 9,
        out_specs=vmem,
        scratch_shapes=[
            pltpu.VMEM((width, DOP + LANES), F32),
            pltpu.VMEM((width, 2 * total), F32),
        ],
        name="map",
    )(windows, cfar_guard.reshape(1, span), cfar_window.reshape(1, span), *tables(total))


def solution(mesh):
    in_specs = (
        P(("chan", "tm"), None, None),
        P("tm", None, None),
        P("tm"),
        P("tm"),
        P("tm"),
        P("tm"),
    )
    out_specs = P(("chan", "tm"), None)
    return jax.shard_map(body, mesh=mesh, in_specs=in_specs, out_specs=out_specs, check_vma=False)
```

profile of v0, /device:TPU:0, one launch (start us, length us, event | category | flops | bytes accessed | tf_op | source)
XLA Modules:
  0.0 29.4 jit_solution(13047411214618618992)
XLA Ops:
  0.0 25.2 %correlate.1.got = f32[8,3,8,128]{3,2,1,0:T(8,128)} custom-call(s32[4]{0:T(128)} %walk_ref.1, s32[4]{0:T(128)} %ids_ref.1, bf16[4,1024,256]{2,1,0:T(8,128)(2,1)} %s_ref.1, bf16[4,1040,256]{2,1,0:T(8,128)(2,1)} %e_ref.1, bf16[256,256]{1,0:T(8,128)(2,1)} %constant.16.clone.swap_ref, bf16[32,256]{1,0:T(8,128)(2,1)} %constant.17.clone.pick_ref), custom_call_target="tpu_custom_call" | custom-call | tf_op jit(solution)/shard_map/correlate/pallas_call | solution.py:252
  25.2 4.2 %map.1 = f32[256,512]{1,0:T(8,128)} custom-call(f32[8,3,8,128]{3,2,1,0:T(8,128)} %correlate.1.got, s32[1,256]{1,0:T(1,128)} %bitcast.2, s32[1,256]{1,0:T(1,128)} %bitcast.3, bf16[512,64]{1,0:T(8,128)(2,1)} %constant.18.clone.dft_high, bf16[512,64]{1,0:T(8,128)(2,1)} %constant.19.clone.dft_low, bf16[64,512]{1,0:T(8,128)(2,1)} %constant.20.clone.tab_high, ...), custom_call_target="tpu_custom_call" | custom-call | tf_op jit(solution)/shard_map/map/pallas_call | solution.py:280
where the time goes:
time: 29.6 us; the launch traced here: 29.4 us
  Pallas kernels  29.4 us (99%)
    pallas_call x1, Pallas kernels, body(): pl.pallas_call(functools.partial(correlate_kernel, span), grid=(blocks,),...  25.2 us
    pallas_call x1, Pallas kernels, body(): pl.pallas_call(functools.partial(map_kernel, span), out_shape=jax.ShapeDt...  4.18 us

commit v1 on v0

v1 whole, which is shorter than its diff:
```python
import functools
import math

import numpy as np
import jax
import jax.numpy as jnp
from jax import lax
from jax.experimental import pallas as pl
from jax.experimental.pallas import tpu as pltpu
from jax.sharding import PartitionSpec as P

D = 2048
DOP = 512
SEGS = 64
GUARD_MAX = 8
WIN_MAX = 16
REACH = GUARD_MAX + WIN_MAX
LANES = 128
SEG_ROWS = D // LANES
CHUNK = SEG_ROWS * SEG_ROWS
MAP_LIMIT = 24 * 1024 * 1024
VMEM_LIMIT = 53 * 1024 * 1024
MESH = pl.DeviceIdType.MESH
F32 = jnp.float32
BF16 = jnp.bfloat16


def window_rows(span):
    return max(s % LANES + span + 2 * REACH for s in range(0, D, span)) // LANES + 1


def iota(shape, dim):
    return lax.broadcasted_iota(jnp.int32, shape, dim)


def split(x):
    high = x.astype(BF16)
    return high, (x - high.astype(F32)).astype(BF16)


def mm(a, b, dims=((1,), (0,))):
    return lax.dot_general(a, b, (dims, ((), ())), preferred_element_type=F32)


def mm3(a, high, low):
    a_high, a_low = split(a)
    return mm(a_high, high) + (mm(a_low, high) + mm(a_high, low))


def correlate_kernel(
    span, walk_hbm, ids_hbm, s_hbm, e_hbm, out_ref,
    walk_ref, ids_ref, s_ref, e_ref, lhs_ref, rhs_ref, diag_ref, send, got,
    small_sem, in_sem, send_sem, recv_sem,
):
    blocks, rows_all = s_hbm.shape[:2]
    chunks = rows_all // CHUNK
    devices = got.shape[0]
    rows_sent = window_rows(span)
    me = lax.axis_index("tm")
    barrier = pltpu.get_barrier_semaphore()
    peers = [lax.rem(me + k, devices) for k in range(1, devices)]
    small = [
        pltpu.make_async_copy(walk_hbm, walk_ref, small_sem.at[0]),
        pltpu.make_async_copy(ids_hbm, ids_ref, small_sem.at[1]),
    ]
    loads = [
        [
            pltpu.make_async_copy(s_hbm.at[j], s_ref.at[j], in_sem.at[j, 0]),
            pltpu.make_async_copy(e_hbm.at[j], e_ref.at[j], in_sem.at[j, 1]),
        ]
        for j in range(blocks)
    ]
    for copy in loads[0] + small + sum(loads[1:], []):
        copy.start()
    for peer in peers:
        pl.semaphore_signal(barrier, inc=1, device_id={"tm": peer}, device_id_type=MESH)
    send[...] = jnp.zeros_like(send)

    def prepare(j):
        slot = j % 2
        for ch in range(chunks):
            at = ch * CHUNK
            lhs_ref[slot, :, at : at + CHUNK] = jnp.transpose(s_ref[j, at : at + CHUNK, :])
        for part in range(2):
            rhs_ref[slot, part] = e_ref[j, :, part * LANES : (part + 1) * LANES].astype(F32)

    def product(j, a):
        slot = j % 2
        off = SEG_ROWS - a
        g = None
        for ch in range(chunks):
            at = ch * CHUNK + off
            rhs = jnp.concatenate([rhs_ref[slot, part, at : at + CHUNK, :] for part in range(2)], 1)
            term = mm(lhs_ref[slot, :, ch * CHUNK : (ch + 1) * CHUNK], rhs.astype(BF16))
            g = term if g is None else g + term
        return (
            g[:LANES, :LANES] + g[LANES:, LANES:],
            g[LANES:, :LANES] - g[:LANES, LANES:],
        )

    lower = iota((LANES, LANES), 1) <= iota((LANES, LANES), 0)

    def fold(j, a, here, later):
        for part in range(2):
            x = jnp.where(lower, here[part], later[part])
            half = LANES // 2
            while half >= 8:
                x = x[:half] + pltpu.roll(x[half:], LANES - half, 1)
                half //= 2
            at = (part * SEG_ROWS + a) * 8
            diag_ref[j % 2, at : at + 8, :] = x

    def finish(j):
        lines = 2 * SEG_ROWS
        x = jnp.concatenate([diag_ref[j % 2, pl.ds(sub, lines, stride=8), :] for sub in range(8)], 1)
        high, low = split(x)
        shift = walk_ref[j] + REACH
        place = iota((8 * LANES, LANES), 0)
        place = place - place // LANES + iota((8 * LANES, LANES), 1) - shift
        turn = jnp.where((place & (LANES - 1)) == 0, 1.0, 0.0).astype(BF16)
        x = mm(jnp.concatenate([high, low], 0), turn)
        x = x[:lines] + x[lines:]
        lane = iota((SEG_ROWS, LANES), 1)
        label = jnp.full((1, LANES), ids_ref[j], jnp.int32).astype(F32)
        zero = jnp.zeros((1, LANES), F32)
        for part in range(2):
            own = x[part * SEG_ROWS : (part + 1) * SEG_ROWS]
            above = jnp.concatenate([zero, own[: SEG_ROWS - 1]], 0)
            tail = jnp.where(lane[:1] < REACH, own[SEG_ROWS - 1 :], 0.0)
            own = jnp.where(lane < shift, above, own)
            for dev in range(devices):
                first = dev * span // LANES
                for r in range(rows_sent):
                    at = first + r
                    row = own[at : at + 1] if at < SEG_ROWS else tail if at == SEG_ROWS else zero
                    to = part * rows_sent + r
                    send[dev, j, to : to + 1, :] = row
        for dev in range(devices):
            send[dev, j, 2 * rows_sent : 2 * rows_sent + 1, :] = label

    def ship(first, count):
        for k, peer in enumerate(peers):
            pltpu.make_async_remote_copy(
                src_ref=send.at[peer, pl.ds(first, count)],
                dst_ref=got.at[me, pl.ds(first, count)],
                send_sem=send_sem.at[k],
                recv_sem=recv_sem.at[k],
                device_id={"tm": peer},
                device_id_type=MESH,
            ).start()

    for copy in loads[0] + small:
        copy.wait()
    prepare(0)
    for j in range(blocks):
        later = product(j, SEG_ROWS)
        for a in reversed(range(SEG_ROWS)):
            here = product(j, a)
            fold(j, a, here, later)
            later = here
            if a == SEG_ROWS - 4 and j > 0:
                finish(j - 1)
            if a == SEG_ROWS // 2 and j == blocks - 1:
                pl.semaphore_wait(barrier, devices - 1)
                ship(0, blocks - 1)
            if a == 4 and j == 0:
                for copy in sum(loads[1:], []):
                    copy.wait()
            if a == 3 and j + 1 < blocks:
                prepare(j + 1)
    finish(blocks - 1)
    ship(blocks - 1, 1)
    got[me] = send[me]
    for k, peer in enumerate(peers):
        pltpu.make_async_copy(send.at[peer], send.at[peer], send_sem.at[k]).wait()
        giver = lax.rem(me + (devices - 1 - k), devices)
        pltpu.make_async_copy(got.at[giver], got.at[giver], recv_sem.at[k]).wait()
    out_ref[...] = got[...].reshape(out_ref.shape)


def cosine(count):
    wrapped = ((count + DOP // 2) & (DOP - 1)) - DOP // 2
    z = (DOP // 4 - jnp.abs(wrapped)).astype(F32) * (2.0 * math.pi / DOP)
    z2 = z * z
    poly = -1.0 / 39916800.0
    for c in (1.0 / 362880.0, -1.0 / 5040.0, 1.0 / 120.0, -1.0 / 6.0, 1.0):
        poly = poly * z2 + c
    return z * poly


def map_kernel(
    span, total, got, guard_ref, size_ref, dft_high, dft_low, tab_high, tab_low, ker_high, ker_low,
    out_ref, power_ref, coef_ref,
):
    me = lax.axis_index("tm")
    rows_sent = window_rows(span)
    pad = got.shape[0] // total
    if span % LANES == 0:
        lead, width = REACH, span + 2 * REACH
    else:
        width = rows_sent * LANES
        lead = pl.multiple_of(lax.rem(me * span, LANES) + REACH, 8)
    guard = guard_ref[...].astype(F32)
    size = size_ref[...].astype(F32)
    guard = jnp.transpose(jnp.broadcast_to(guard, (LANES, span)))
    outer = guard + jnp.transpose(jnp.broadcast_to(size, (LANES, span)))
    dist = iota((span, LANES), 1).astype(F32)
    inside = jnp.where((dist > guard) & (dist <= outer), 1.0, 0.0).astype(BF16)
    kernel = mm(inside, ker_high[...]) + mm(inside, ker_low[...])
    guard, outer = guard[:, :1], outer[:, :1]
    dist = jnp.abs(iota((span, width), 1) - lead - iota((span, width), 0)).astype(F32)
    band = jnp.where((dist > guard) & (dist <= outer), 1.0, 0.0).astype(BF16)
    spot = (me * span + iota((span, 1), 0)).astype(F32)
    last = (D - 1) - spot
    count = jnp.minimum(spot, outer) - jnp.minimum(spot, guard)
    count = count + jnp.minimum(last, outer) - jnp.minimum(last, guard)
    weight = 1.0 / (count + 2.0 * (outer - guard))

    def lines(at):
        return got[pl.ds(at, total, stride=pad), :]

    parts = [jnp.concatenate([lines(part * rows_sent + r) for r in range(rows_sent)], 1) for part in range(2)]
    stacked = jnp.concatenate(parts, 0)
    ids = lines(2 * rows_sent)[:, :1].astype(jnp.int32)
    turns = ids * iota((total, DOP), 1)
    cos_high, cos_low = split(cosine(turns))
    sin_high, sin_low = split(cosine(turns - DOP // 4))
    mix_re_high = jnp.concatenate([cos_high, sin_high], 0)
    mix_re_low = jnp.concatenate([cos_low, sin_low], 0)
    mix_im_high = jnp.concatenate([-sin_high, cos_high], 0)
    mix_im_low = jnp.concatenate([-sin_low, cos_low], 0)
    corr = jnp.transpose(stacked)[:width]
    corr_high, corr_low = split(corr)
    norm = 1.0 / (total * SEGS * D)
    re = mm(corr_high, mix_re_high) + (mm(corr_low, mix_re_high) + mm(corr_high, mix_re_low))
    im = mm(corr_high, mix_im_high) + (mm(corr_low, mix_im_high) + mm(corr_high, mix_im_low))
    power = (re * re + im * im) * norm
    floor = jnp.sum(corr * corr, axis=1, keepdims=True) * norm
    coef = mm3(power, dft_high[...], dft_low[...])
    if span % LANES == 0:
        power_c = power[lead : lead + span]
        coef_c = coef[lead : lead + span]
        floor_c = floor[lead : lead + span]
    else:
        power_ref[:, :DOP] = power
        power_ref[:, DOP:] = jnp.broadcast_to(floor, (width, LANES))
        coef_ref[...] = coef
        power_c = power_ref[pl.ds(lead, span), :DOP]
        floor_c = power_ref[pl.ds(lead, span), DOP:][:, :1]
        coef_c = coef_ref[pl.ds(lead, span), :]
    coef_high, coef_low = split(coef)
    sums = mm(band, coef_high) + mm(band, coef_low) + coef_c * kernel
    noise = mm3(sums, tab_high[...], tab_low[...]) * weight
    out_ref[...] = (power_c - floor_c) / (0.25 + noise)


def np_split(x):
    high = x.astype(BF16)
    return jnp.asarray(high), jnp.asarray((x - high.astype(np.float64)).astype(BF16))


def tables(total):
    lag, freq = np.arange(total), np.arange(DOP)
    angle = 2.0 * np.pi / DOP * ((lag[:, None] * freq[None, :]) % DOP)
    tab = np.concatenate([np.cos(angle), np.sin(angle)], 0)
    scale = np.where(lag == 0, 1.0, 2.0) / DOP
    dft = tab.T * np.concatenate([scale, scale])[None, :]
    dist = np.arange(LANES)
    ker = 2.0 * np.cos(2.0 * np.pi / DOP * ((dist[:, None] * lag[None, :]) % DOP))
    ker = np.concatenate([ker, ker], 1)
    return (*np_split(dft), *np_split(tab), *np_split(ker))


def body(surveillance, ref_samples, block_ids, walk, cfar_guard, cfar_window):
    blocks, rows_all = surveillance.shape[:2]
    devices = lax.axis_size("tm")
    total = blocks * devices
    span = D // devices
    rows_sent = window_rows(span)
    pad = -(-(2 * rows_sent + 1) // 8) * 8
    send_shape = (devices, blocks, pad, LANES)
    vmem = pl.BlockSpec(memory_space=pltpu.VMEM)
    hbm = pl.BlockSpec(memory_space=pltpu.HBM)
    windows = pl.pallas_call(
        functools.partial(correlate_kernel, span),
        out_shape=jax.ShapeDtypeStruct((total * pad, LANES), F32),
        in_specs=[hbm] * 4,
        out_specs=vmem,
        scratch_shapes=[
            pltpu.SMEM((blocks,), jnp.int32),
            pltpu.SMEM((blocks,), jnp.int32),
            pltpu.VMEM(surveillance.shape, BF16),
            pltpu.VMEM(ref_samples.shape, BF16),
            pltpu.VMEM((2, 2 * LANES, rows_all), BF16),
            pltpu.VMEM((2, 2, ref_samples.shape[1], LANES), F32),
            pltpu.VMEM((2, 2 * SEG_ROWS * 8, LANES), F32),
            pltpu.VMEM(send_shape, F32),
            pltpu.VMEM(send_shape, F32),
            pltpu.SemaphoreType.DMA((2,)),
            pltpu.SemaphoreType.DMA((blocks, 2)),
            pltpu.SemaphoreType.DMA((devices,)),
            pltpu.SemaphoreType.DMA((devices,)),
        ],
        compiler_params=pltpu.CompilerParams(
            collective_id=0, has_side_effects=True, vmem_limit_bytes=VMEM_LIMIT
        ),
        name="correlate",
    )(walk, block_ids, surveillance, ref_samples)
    width = span + 2 * REACH if span % LANES == 0 else rows_sent * LANES
    return pl.pallas_call(
        functools.partial(map_kernel, span, total),
        out_shape=jax.ShapeDtypeStruct((span, DOP), F32),
        in_specs=[vmem] * 9,
        out_specs=vmem,
        scratch_shapes=[
            pltpu.VMEM((width, DOP + LANES), F32),
            pltpu.VMEM((width, 2 * total), F32),
        ],
        compiler_params=pltpu.CompilerParams(vmem_limit_bytes=MAP_LIMIT),
        name="map",
    )(windows, cfar_guard.reshape(1, span), cfar_window.reshape(1, span), *tables(total))


def solution(mesh):
    in_specs = (
        P(("chan", "tm"), None, None),
        P("tm", None, None),
        P("tm"),
        P("tm"),
        P("tm"),
        P("tm"),
    )
    out_specs = P(("chan", "tm"), None)
    return jax.shard_map(body, mesh=mesh, in_specs=in_specs, out_specs=out_specs, check_vma=False)
```

time: 29.6 us -> 25.4 us (0.86)
  Pallas kernels: 29.4 us -> 23.8 us
  local copies, waits for them, and re-layouts: 0 us -> 1.35 us
    pallas_call x2, Pallas kernels: 29.4 us -> 23.8 us  [the longest x1 20.7 us: body(): pl.pallas_call(functools.partial(correlate_kernel, span), out_shape=jax.S...]
    unnamed x0 -> x20, local copies, waits for them, and re-layouts: none -> 1.35 us
where the time goes in v1:
time: 25.4 us; the launch traced here: 25.2 us
  Pallas kernels  23.8 us (94%)
  local copies, waits for them, and re-layouts  1.35 us (5%)
    pallas_call x1, Pallas kernels, body(): pl.pallas_call(functools.partial(correlate_kernel, span), out_shape=jax.S...  20.7 us
    pallas_call x1, Pallas kernels, body(): pl.pallas_call(functools.partial(map_kernel, span, total), out_shape=jax....  3.04 us
    unnamed x20, local copies, waits for them, and re-layouts  1.35 us

profile of v1, /device:TPU:0, one launch (start us, length us, event | category | flops | bytes accessed | tf_op | source)
XLA Modules:
  0.0 25.2 jit_solution(590620791027272743)
XLA Ops:
  0.0 0.0 copy-start.8
  0.0 0.7 %copy-done.8 = s32[4]{0:T(128)S(1)} copy-done((s32[4]{0:T(128)S(1)}, s32[4]{0:T(128)}, u32[]{:S(2)}) %copy-start.8) | copy-done | bytes 40
  0.7 0.0 copy-start.9
  0.7 0.7 %copy-done.9 = s32[4]{0:T(128)S(1)} copy-done((s32[4]{0:T(128)S(1)}, s32[4]{0:T(128)}, u32[]{:S(2)}) %copy-start.9) | copy-done | bytes 40
  1.3 0.0 copy-start
  1.3 0.0 copy-start.1
  1.3 0.0 copy-start.2
  1.3 0.0 copy-start.3
  1.3 0.0 copy-start.4
  1.3 0.0 copy-start.5
  1.3 0.0 copy-start.6
  1.4 0.0 copy-start.7
  1.4 20.7 %correlate.1.got = f32[256,128]{1,0:T(8,128)S(1)} custom-call(s32[4]{0:T(128)S(1)} %copy-done.8, s32[4]{0:T(128)S(1)} %copy-done.9, bf16[4,1024,256]{2,1,0:T(8,128)(2,1)} %s_hbm.1, bf16[4,1040,256]{2,1,0:T(8,128)(2,1)} %e_hbm.1), custom_call_target="tpu_custom_call" | custom-call | tf_op jit(solution)/shard_map/correlate/pallas_call | solution.py:284
  22.1 0.0 copy-done
  22.1 0.0 copy-done.1
  22.1 0.0 copy-done.2
  22.1 0.0 copy-done.3
  22.1 0.0 copy-done.4
  22.1 0.0 copy-done.5
  22.1 0.0 copy-done.6
  22.2 0.0 copy-done.7
  22.2 3.0 %map.1 = f32[256,512]{1,0:T(8,128)} custom-call(f32[256,128]{1,0:T(8,128)S(1)} %correlate.1.got, s32[1,256]{1,0:T(1,128)S(1)} %bitcast.2, s32[1,256]{1,0:T(1,128)S(1)} %bitcast.3, bf16[512,64]{1,0:T(8,128)(2,1)S(1)} %copy-done.1, bf16[512,64]{1,0:T(8,128)(2,1)S(1)} %copy-done, bf16[64,512]{1,0:T(8,128)(2,1)S(1)} %copy-done.3, bf16[64,512]{1,0:T(8,128)(2,1)S(1)} %copy-done.2, ...), custom_call_target="tpu_custom_call" | custom-call | tf_op jit(solution)/shard_map/map/pallas_call | solution.py:310
Async XLA Ops:
  0.0 0.7 %copy-start.8 = (s32[4]{0:T(128)S(1)}, s32[4]{0:T(128)}, u32[]{:S(2)}) copy-start(s32[4]{0:T(128)} %walk_hbm.1) | copy-start | bytes 52
  0.7 0.7 %copy-start.9 = (s32[4]{0:T(128)S(1)}, s32[4]{0:T(128)}, u32[]{:S(2)}) copy-start(s32[4]{0:T(128)} %ids_hbm.1) | copy-start | bytes 52
  1.3 20.8 %copy-start = (bf16[512,64]{1,0:T(8,128)(2,1)S(1)}, bf16[512,64]{1,0:T(8,128)(2,1)}, u32[]{:S(2)}) copy-start(bf16[512,64]{1,0:T(8,128)(2,1)} %constant.13.clone.dft_low) | copy-start | bytes 196612
  1.3 20.8 %copy-start.1 = (bf16[512,64]{1,0:T(8,128)(2,1)S(1)}, bf16[512,64]{1,0:T(8,128)(2,1)}, u32[]{:S(2)}) copy-start(bf16[512,64]{1,0:T(8,128)(2,1)} %constant.12.clone.dft_high) | copy-start | bytes 196612
  1.3 20.8 %copy-start.2 = (bf16[64,512]{1,0:T(8,128)(2,1)S(1)}, bf16[64,512]{1,0:T(8,128)(2,1)}, u32[]{:S(2)}) copy-start(bf16[64,512]{1,0:T(8,128)(2,1)} %constant.15.clone.tab_low) | copy-start | bytes 196612
  1.3 20.8 %copy-start.3 = (bf16[64,512]{1,0:T(8,128)(2,1)S(1)}, bf16[64,512]{1,0:T(8,128)(2,1)}, u32[]{:S(2)}) copy-start(bf16[64,512]{1,0:T(8,128)(2,1)} %constant.14.clone.tab_high) | copy-start | bytes 196612
  1.3 20.8 %copy-start.4 = (bf16[128,64]{1,0:T(8,128)(2,1)S(1)}, bf16[128,64]{1,0:T(8,128)(2,1)}, u32[]{:S(2)}) copy-start(bf16[128,64]{1,0:T(8,128)(2,1)} %constant.17.clone.ker_low) | copy-start | bytes 49156
  1.3 20.8 %copy-start.5 = (bf16[128,64]{1,0:T(8,128)(2,1)S(1)}, bf16[128,64]{1,0:T(8,128)(2,1)}, u32[]{:S(2)}) copy-start(bf16[128,64]{1,0:T(8,128)(2,1)} %constant.16.clone.ker_high) | copy-start | bytes 49156
  1.3 20.8 %copy-start.6 = (s32[256]{0:T(256)S(1)}, s32[256]{0:T(256)}, u32[]{:S(2)}) copy-start(s32[256]{0:T(256)} %param.16) | copy-start | bytes 3076
  1.4 20.8 %copy-start.7 = (s32[256]{0:T(256)S(1)}, s32[256]{0:T(256)}, u32[]{:S(2)}) copy-start(s32[256]{0:T(256)} %param.17) | copy-start | bytes 3076

commit v2 on v1

v2 whole, which is shorter than its diff:
```python
import functools
import math

import numpy as np
import jax
import jax.numpy as jnp
from jax import lax
from jax.experimental import pallas as pl
from jax.experimental.pallas import tpu as pltpu
from jax.sharding import PartitionSpec as P

D = 2048
DOP = 512
SEGS = 64
GUARD_MAX = 8
WIN_MAX = 16
REACH = GUARD_MAX + WIN_MAX
LANES = 128
SEG_ROWS = D // LANES
CHUNK = SEG_ROWS * SEG_ROWS
GROUPS = 4
FINISH_AT = 3
SHIP_AT = 5
LAND_AT = 7
LINES = SEG_ROWS + 8
MAP_LIMIT = 24 * 1024 * 1024
VMEM_LIMIT = 53 * 1024 * 1024
MESH = pl.DeviceIdType.MESH
F32 = jnp.float32
BF16 = jnp.bfloat16


def window_rows(span):
    return max(s % LANES + span + 2 * REACH for s in range(0, D, span)) // LANES + 1


def iota(shape, dim):
    return lax.broadcasted_iota(jnp.int32, shape, dim)


def split(x):
    high = x.astype(BF16)
    return high, (x - high.astype(F32)).astype(BF16)


def mm(a, b, dims=((1,), (0,))):
    return lax.dot_general(a, b, (dims, ((), ())), preferred_element_type=F32)


def correlate_kernel(
    span, walk_hbm, ids_hbm, s_hbm, e_hbm, out_ref,
    walk_ref, ids_ref, s_ref, e_ref, lhs_ref, rhs_ref, hold_ref, diag_ref, send, got,
    small_sem, piece_sem, in_sem, send_sem, recv_sem,
):
    blocks, rows_all = s_hbm.shape[:2]
    chunks = rows_all // CHUNK
    devices = got.shape[0]
    rows_sent = window_rows(span)
    group_rows = SEG_ROWS // GROUPS
    per = devices // GROUPS
    me = lax.axis_index("tm")
    barrier = pltpu.get_barrier_semaphore()
    peers = [lax.rem(me + k, devices) for k in range(1, devices)]
    small = [
        pltpu.make_async_copy(walk_hbm, walk_ref, small_sem.at[0]),
        pltpu.make_async_copy(ids_hbm, ids_ref, small_sem.at[1]),
    ]
    loads = [
        [
            pltpu.make_async_copy(s_hbm.at[j], s_ref.at[j], in_sem.at[j, 0]),
            pltpu.make_async_copy(e_hbm.at[j], e_ref.at[j], in_sem.at[j, 1]),
        ]
        for j in range(1, blocks)
    ]
    pieces = []
    for ch in range(chunks):
        rows = pl.ds(ch * CHUNK, CHUNK)
        tail = pl.ds(ch * CHUNK, CHUNK + (SEG_ROWS if ch == chunks - 1 else 0))
        pieces.append(
            [
                pltpu.make_async_copy(s_hbm.at[0, rows], s_ref.at[0, rows], piece_sem.at[ch, 0]),
                pltpu.make_async_copy(e_hbm.at[0, tail], e_ref.at[0, tail], piece_sem.at[ch, 1]),
            ]
        )
    for copy in sum(pieces, []) + small + sum(loads, []):
        copy.start()
    for peer in peers:
        pl.semaphore_signal(barrier, inc=1, device_id={"tm": peer}, device_id_type=MESH)
    send[...] = jnp.zeros_like(send)
    diag_ref[...] = jnp.zeros_like(diag_ref)

    def prepare_chunk(j, ch):
        at = ch * CHUNK
        flip = jnp.transpose(s_ref[j, at : at + CHUNK, :])
        lhs_ref[j, 2 * ch] = flip[:, :LANES]
        lhs_ref[j, 2 * ch + 1] = flip[:, LANES:]
        end = at + CHUNK + (SEG_ROWS if ch == chunks - 1 else 0)
        for part in range(2):
            rhs_ref[j, part, at:end, :] = e_ref[j, at:end, part * LANES : (part + 1) * LANES].astype(F32)

    def prepare(j):
        for ch in range(chunks):
            prepare_chunk(j, ch)

    def product(j, a):
        off = SEG_ROWS - a
        g = None
        for ch in range(chunks):
            at = ch * CHUNK + off
            rhs = jnp.concatenate([rhs_ref[j, part, at : at + CHUNK, :] for part in range(2)], 1)
            lhs = jnp.concatenate([lhs_ref[j, 2 * ch], lhs_ref[j, 2 * ch + 1]], 1)
            term = mm(lhs, rhs.astype(BF16))
            g = term if g is None else g + term
        return g

    def fold(j, step, g):
        totals = [None, None]
        for i in range(0, LANES, 8):
            k = LANES + i
            pair = (
                g[i : i + 8, :LANES] + g[k : k + 8, LANES:],
                g[k : k + 8, :LANES] - g[i : i + 8, LANES:],
            )
            low = iota((8, LANES), 1) <= iota((8, LANES), 0) + i
            for part in range(2):
                if step > 0:
                    prev = hold_ref[j, part, i : i + 8, :]
                    x = jnp.where(low, prev, pair[part])
                    x = pltpu.roll(x, LANES - i, 1) if i else x
                    totals[part] = x if totals[part] is None else totals[part] + x
                if step < SEG_ROWS:
                    hold_ref[j, part, i : i + 8, :] = pair[part]
        if step > 0:
            for part in range(2):
                x = totals[part]
                for half in (4, 2, 1):
                    x = x + pltpu.roll(pltpu.roll(x, 8 - half, 0), LANES - half, 1)
                diag_ref[j, part, step * 8 : step * 8 + 8, :] = x

    def run(j, step):
        fold(j, step, product(j, step))

    def finish(group, count, chosen):
        lines = -(-(count * group_rows + 2) // 8) * 8
        base = group * group_rows
        late_by = (LANES - iota((lines, LANES), 1)) & (LANES - 1)
        place = (iota((lines, LANES), 0) + base) * LANES + late_by
        for j in chosen:
            shift = walk_ref[j] + REACH
            label = jnp.full((1, LANES), ids_ref[j], jnp.int32).astype(F32)
            for part in range(2):
                y = diag_ref[j, part, pl.ds(base * 8, lines, stride=8), :]
                y = pltpu.roll(y, LANES - shift, 1)
                y = jnp.where(late_by < shift, y, pltpu.roll(y, lines - 1, 0))
                y = jnp.where(place < D + REACH, y, 0.0)
                for e in range(per * count):
                    top = e * span // LANES
                    to = part * rows_sent
                    send[group * per + e, j, to : to + rows_sent, :] = y[top : top + rows_sent]
            for e in range(per * count):
                send[group * per + e, j, 2 * rows_sent : 2 * rows_sent + 1, :] = label

    def ship(group, first, count):
        for dev in range(group * per, (group + 1) * per):

            @pl.when(dev != me)
            def _():
                pltpu.make_async_remote_copy(
                    src_ref=send.at[dev, pl.ds(first, count)],
                    dst_ref=got.at[me, pl.ds(first, count)],
                    send_sem=send_sem.at[dev],
                    recv_sem=recv_sem.at[me],
                    device_id={"tm": dev},
                    device_id_type=MESH,
                ).start()

    for ch in range(chunks):
        for copy in pieces[ch]:
            copy.wait()
        prepare_chunk(0, ch)
    for copy in small:
        copy.wait()
    ends = [group_rows * (k + 1) + 2 for k in range(GROUPS)]
    ends[-1] = SEG_ROWS + 1
    late = list(range(max(blocks - 2, 0), blocks))
    early = list(range(late[0]))
    jobs = []
    for j in early:
        for step in range(SEG_ROWS + 1):
            jobs.append((j, step))
    marks = []
    for k in range(GROUPS):
        for j in late:
            for step in range(ends[k - 1] if k else 0, ends[k]):
                jobs.append((j, step))
        marks.append(len(jobs))

    def deliver(k):
        if k == 0:
            pl.semaphore_wait(barrier, devices - 1)
            ship(0, 0, blocks)
            for group in range(1, GROUPS):
                ship(group, 0, len(early))
        elif k < GROUPS - 2:
            ship(k, late[0], len(late))
        elif k == GROUPS - 2:
            ship(k, late[0], len(late))
            ship(k + 1, late[0], len(late) - 1)
        else:
            ship(k, blocks - 1, 1)

    when = {}

    def plan(at, what):
        when.setdefault(at, []).append(what)

    def land():
        for copy in sum(loads, []):
            copy.wait()
        prepare(1)

    plan(LAND_AT, land)
    for j in range(2, blocks):
        plan((SEG_ROWS + 1) * (j - 2) + SEG_ROWS, functools.partial(prepare, j))
    if early:
        plan(marks[0] - 2, functools.partial(finish, 0, GROUPS, early))
    for k in range(GROUPS - 1):
        plan(marks[k] + FINISH_AT, functools.partial(finish, k, 1, late))
        if k < GROUPS - 2:
            plan(marks[k] + SHIP_AT, functools.partial(deliver, k))
    plan(len(jobs) - 3, functools.partial(finish, GROUPS - 1, 1, late[:-1]))
    plan(len(jobs) - 1, functools.partial(deliver, GROUPS - 2))
    for n, (j, step) in enumerate(jobs):
        run(j, step)
        for what in when.get(n + 1, []):
            what()
    finish(GROUPS - 1, 1, late[-1:])
    deliver(GROUPS - 1)
    got[me] = send[me]
    for peer in peers:
        pltpu.make_async_copy(send.at[peer], send.at[peer], send_sem.at[peer]).wait()
        pltpu.make_async_copy(got.at[peer], got.at[peer], recv_sem.at[peer]).wait()
    out_ref[...] = got[...].reshape(out_ref.shape)


def cosine(count):
    wrapped = ((count + DOP // 2) & (DOP - 1)) - DOP // 2
    z = (DOP // 4 - jnp.abs(wrapped)).astype(F32) * (2.0 * math.pi / DOP)
    z2 = z * z
    poly = -1.0 / 39916800.0
    for c in (1.0 / 362880.0, -1.0 / 5040.0, 1.0 / 120.0, -1.0 / 6.0, 1.0):
        poly = poly * z2 + c
    return z * poly


def map_kernel(
    span, total, got, guard_ref, size_ref, dft, tab, ker,
    out_ref, power_ref, coef_ref,
):
    me = lax.axis_index("tm")
    rows_sent = window_rows(span)
    pad = got.shape[0] // total
    if span % LANES == 0:
        lead, width = REACH, span + 2 * REACH
    else:
        width = rows_sent * LANES
        lead = pl.multiple_of(lax.rem(me * span, LANES) + REACH, 8)
    guard = guard_ref[...].astype(F32)
    size = size_ref[...].astype(F32)
    guard = jnp.transpose(jnp.broadcast_to(guard, (LANES, span)))
    outer = guard + jnp.transpose(jnp.broadcast_to(size, (LANES, span)))
    dist = iota((span, LANES), 1).astype(F32)
    inside = jnp.where((dist > guard) & (dist <= outer), 1.0, 0.0).astype(BF16)
    kernel = mm(inside, ker[...])
    kernel = kernel[:, : 2 * total] + kernel[:, 2 * total :]
    guard, outer = guard[:, :1], outer[:, :1]
    dist = jnp.abs(iota((span, width), 1) - lead - iota((span, width), 0)).astype(F32)
    band = jnp.where((dist > guard) & (dist <= outer), 1.0, 0.0).astype(BF16)
    spot = (me * span + iota((span, 1), 0)).astype(F32)
    last = (D - 1) - spot
    count = jnp.minimum(spot, outer) - jnp.minimum(spot, guard)
    count = count + jnp.minimum(last, outer) - jnp.minimum(last, guard)
    weight = 1.0 / (count + 2.0 * (outer - guard))

    def lines(at):
        return got[pl.ds(at, total, stride=pad), :]

    parts = [jnp.concatenate([lines(part * rows_sent + r) for r in range(rows_sent)], 1) for part in range(2)]
    stacked = jnp.concatenate(split(jnp.concatenate(parts, 0)), 0)
    turn = jnp.where(((iota((LANES, LANES), 0) + iota((LANES, LANES), 1)) & (LANES - 1)) == 0, 1.0, 0.0)
    turn = turn.astype(BF16)
    corr = [mm(turn, stacked[:, r * LANES : (r + 1) * LANES], ((1,), (1,))) for r in range(rows_sent)]
    corr = jnp.concatenate(corr, 0)[:width]
    both = corr.astype(BF16)
    both = jnp.concatenate([both, both[:, : 2 * total]], 1)
    ids = lines(2 * rows_sent)[:, :1].astype(jnp.int32)
    turns = ids * iota((total, DOP), 1)
    cos_high, cos_low = split(cosine(turns))
    sin_high, sin_low = split(cosine(turns - DOP // 4))
    mix_re = jnp.concatenate([cos_high, sin_high, cos_high, sin_high, cos_low, sin_low], 0)
    mix_im = jnp.concatenate([-sin_high, cos_high, -sin_high, cos_high, -sin_low, cos_low], 0)
    norm = 1.0 / (total * SEGS * D)
    re = mm(both, mix_re)
    im = mm(both, mix_im)
    power = (re * re + im * im) * norm
    corr = corr[:, : 2 * total] + corr[:, 2 * total :]
    floor = jnp.sum(corr * corr, axis=1, keepdims=True) * norm
    high, low = split(power)
    coef = mm(high, dft[...])
    coef = coef[:, : 2 * total] + coef[:, 2 * total :] + mm(low, dft[:, : 2 * total])
    if span % LANES == 0:
        power_c = power[lead : lead + span]
        coef_c = coef[lead : lead + span]
        floor_c = floor[lead : lead + span]
    else:
        power_ref[:, :DOP] = power
        power_ref[:, DOP:] = jnp.broadcast_to(floor, (width, LANES))
        coef_ref[...] = coef
        power_c = power_ref[pl.ds(lead, span), :DOP]
        floor_c = power_ref[pl.ds(lead, span), DOP:][:, :1]
        coef_c = coef_ref[pl.ds(lead, span), :]
    sums = mm(band, jnp.concatenate(split(coef), 1))
    sums = sums[:, : 2 * total] + sums[:, 2 * total :] + coef_c * kernel
    high, low = split(sums)
    noise = mm(jnp.concatenate([high, low, high], 1), tab[...]) * weight
    out_ref[...] = (power_c - floor_c) / (0.25 + noise)


def np_split(x):
    high = x.astype(BF16)
    return high, (x - high.astype(np.float64)).astype(BF16)


def tables(total):
    lag, freq = np.arange(total), np.arange(DOP)
    angle = 2.0 * np.pi / DOP * ((lag[:, None] * freq[None, :]) % DOP)
    tab = np.concatenate([np.cos(angle), np.sin(angle)], 0)
    scale = np.where(lag == 0, 1.0, 2.0) / DOP
    dft = tab.T * np.concatenate([scale, scale])[None, :]
    dist = np.arange(LANES)
    ker = 2.0 * np.cos(2.0 * np.pi / DOP * ((dist[:, None] * lag[None, :]) % DOP))
    ker = np.concatenate([ker, ker], 1)
    high, low = np_split(tab)
    stacks = np.concatenate(np_split(dft), 1), np.concatenate([high, high, low], 0), np.concatenate(np_split(ker), 1)
    return [jnp.asarray(stack) for stack in stacks]


def body(surveillance, ref_samples, block_ids, walk, cfar_guard, cfar_window):
    blocks, rows_all = surveillance.shape[:2]
    devices = lax.axis_size("tm")
    total = blocks * devices
    span = D // devices
    rows_sent = window_rows(span)
    pad = -(-(2 * rows_sent + 1) // 8) * 8
    send_shape = (devices, blocks, pad, LANES)
    vmem = pl.BlockSpec(memory_space=pltpu.VMEM)
    hbm = pl.BlockSpec(memory_space=pltpu.HBM)
    windows = pl.pallas_call(
        functools.partial(correlate_kernel, span),
        out_shape=jax.ShapeDtypeStruct((total * pad, LANES), F32),
        in_specs=[hbm] * 4,
        out_specs=vmem,
        scratch_shapes=[
            pltpu.SMEM((blocks,), jnp.int32),
            pltpu.SMEM((blocks,), jnp.int32),
            pltpu.VMEM(surveillance.shape, BF16),
            pltpu.VMEM(ref_samples.shape, BF16),
            pltpu.VMEM((blocks, rows_all // LANES, 2 * LANES, LANES), BF16),
            pltpu.VMEM((blocks, 2, ref_samples.shape[1], LANES), F32),
            pltpu.VMEM((blocks, 2, LANES, LANES), F32),
            pltpu.VMEM((blocks, 2, LINES * 8, LANES), F32),
            pltpu.VMEM(send_shape, F32),
            pltpu.VMEM(send_shape, F32),
            pltpu.SemaphoreType.DMA((2,)),
            pltpu.SemaphoreType.DMA((rows_all // CHUNK, 2)),
            pltpu.SemaphoreType.DMA((blocks, 2)),
            pltpu.SemaphoreType.DMA((devices,)),
            pltpu.SemaphoreType.DMA((devices,)),
        ],
        compiler_params=pltpu.CompilerParams(
            collective_id=0, has_side_effects=True, vmem_limit_bytes=VMEM_LIMIT
        ),
        name="correlate",
    )(walk, block_ids, surveillance, ref_samples)
    width = span + 2 * REACH if span % LANES == 0 else rows_sent * LANES
    return pl.pallas_call(
        functools.partial(map_kernel, span, total),
        out_shape=jax.ShapeDtypeStruct((span, DOP), F32),
        in_specs=[vmem] * 6,
        out_specs=vmem,
        scratch_shapes=[
            pltpu.VMEM((width, DOP + LANES), F32),
            pltpu.VMEM((width, 2 * total), F32),
        ],
        compiler_params=pltpu.CompilerParams(vmem_limit_bytes=MAP_LIMIT),
        name="map",
    )(windows, cfar_guard.reshape(1, span), cfar_window.reshape(1, span), *tables(total))


def solution(mesh):
    in_specs = (
        P(("chan", "tm"), None, None),
        P("tm", None, None),
        P("tm"),
        P("tm"),
        P("tm"),
        P("tm"),
    )
    out_specs = P(("chan", "tm"), None)
    return jax.shard_map(body, mesh=mesh, in_specs=in_specs, out_specs=out_specs, check_vma=False)
```

time: 25.4 us -> 21.5 us (0.85)
  Pallas kernels: 23.8 us -> 19.9 us
    pallas_call x1, Pallas kernels: 20.7 us -> 17.6 us  [body(): pl.pallas_call(functools.partial(correlate_kernel, span), out_shape=jax.S...]
    pallas_call x1, Pallas kernels: 3.04 us -> 2.35 us  [body(): pl.pallas_call(functools.partial(map_kernel, span, total), out_shape=jax....]
    unnamed x20 -> x14, local copies, waits for them, and re-layouts: 1.35 us -> 1.33 us
where the time goes in v2:
time: 21.5 us; the launch traced here: 21.3 us
  Pallas kernels  19.9 us (93%)
  local copies, waits for them, and re-layouts  1.33 us (6%)
    pallas_call x1, Pallas kernels, body(): pl.pallas_call(functools.partial(correlate_kernel, span), out_shape=jax.S...  17.6 us
    pallas_call x1, Pallas kernels, body(): pl.pallas_call(functools.partial(map_kernel, span, total), out_shape=jax....  2.35 us
    unnamed x14, local copies, waits for them, and re-layouts  1.33 us

profile of v2, /device:TPU:0, one launch (start us, length us, event | category | flops | bytes accessed | tf_op | source)
XLA Modules:
  0.0 21.3 jit_solution(8102799790606638256)
XLA Ops:
  0.0 0.0 copy-start.5
  0.0 0.7 %copy-done.5 = s32[4]{0:T(128)S(1)} copy-done((s32[4]{0:T(128)S(1)}, s32[4]{0:T(128)}, u32[]{:S(2)}) %copy-start.5) | copy-done | bytes 40
  0.7 0.0 copy-start.6
  0.7 0.7 %copy-done.6 = s32[4]{0:T(128)S(1)} copy-done((s32[4]{0:T(128)S(1)}, s32[4]{0:T(128)}, u32[]{:S(2)}) %copy-start.6) | copy-done | bytes 40
  1.3 0.0 copy-start
  1.3 0.0 copy-start.1
  1.3 0.0 copy-start.2
  1.3 0.0 copy-start.3
  1.3 0.0 copy-start.4
  1.3 17.6 %correlate.1.got = f32[256,128]{1,0:T(8,128)S(1)} custom-call(s32[4]{0:T(128)S(1)} %copy-done.5, s32[4]{0:T(128)S(1)} %copy-done.6, bf16[4,1024,256]{2,1,0:T(8,128)(2,1)} %s_hbm.1, bf16[4,1040,256]{2,1,0:T(8,128)(2,1)} %e_hbm.1), custom_call_target="tpu_custom_call" | custom-call | tf_op jit(solution)/shard_map/correlate/pallas_call | solution.py:358
  18.9 0.0 copy-done
  18.9 0.0 copy-done.1
  18.9 0.0 copy-done.2
  18.9 0.0 copy-done.3
  19.0 0.0 copy-done.4
  19.0 2.3 %map.1 = f32[256,512]{1,0:T(8,128)} custom-call(f32[256,128]{1,0:T(8,128)S(1)} %correlate.1.got, s32[1,256]{1,0:T(1,128)S(1)} %bitcast.2, s32[1,256]{1,0:T(1,128)S(1)} %bitcast.3, bf16[512,128]{1,0:T(8,128)(2,1)S(1)} %copy-done.1, bf16[192,512]{1,0:T(8,128)(2,1)S(1)} %copy-done, bf16[128,128]{1,0:T(8,128)(2,1)S(1)} %copy-done.2), custom_call_target="tpu_custom_call" | custom-call | tf_op jit(solution)/shard_map/map/pallas_call | solution.py:386
Async XLA Ops:
  0.0 0.7 %copy-start.5 = (s32[4]{0:T(128)S(1)}, s32[4]{0:T(128)}, u32[]{:S(2)}) copy-start(s32[4]{0:T(128)} %walk_hbm.1) | copy-start | bytes 52
  0.7 0.7 %copy-start.6 = (s32[4]{0:T(128)S(1)}, s32[4]{0:T(128)}, u32[]{:S(2)}) copy-start(s32[4]{0:T(128)} %ids_hbm.1) | copy-start | bytes 52
  1.3 17.6 %copy-start = (bf16[192,512]{1,0:T(8,128)(2,1)S(1)}, bf16[192,512]{1,0:T(8,128)(2,1)}, u32[]{:S(2)}) copy-start(bf16[192,512]{1,0:T(8,128)(2,1)} %constant.7.clone.tab) | copy-start | bytes 589828
  1.3 17.6 %copy-start.1 = (bf16[512,128]{1,0:T(8,128)(2,1)S(1)}, bf16[512,128]{1,0:T(8,128)(2,1)}, u32[]{:S(2)}) copy-start(bf16[512,128]{1,0:T(8,128)(2,1)} %constant.6.clone.dft) | copy-start | bytes 393220
  1.3 17.6 %copy-start.2 = (bf16[128,128]{1,0:T(8,128)(2,1)S(1)}, bf16[128,128]{1,0:T(8,128)(2,1)}, u32[]{:S(2)}) copy-start(bf16[128,128]{1,0:T(8,128)(2,1)} %constant.8.clone.ker) | copy-start | bytes 98308
  1.3 17.6 %copy-start.3 = (s32[256]{0:T(256)S(1)}, s32[256]{0:T(256)}, u32[]{:S(2)}) copy-start(s32[256]{0:T(256)} %param.13) | copy-start | bytes 3076
  1.3 17.6 %copy-start.4 = (s32[256]{0:T(256)S(1)}, s32[256]{0:T(256)}, u32[]{:S(2)}) copy-start(s32[256]{0:T(256)} %param.14) | copy-start | bytes 3076

commit v3 on v2

--- a/solution.py
+++ b/solution.py
@@ -19,6 +19,7 @@
 SEG_ROWS = D // LANES
 CHUNK = SEG_ROWS * SEG_ROWS
 GROUPS = 4
+PIECES = 4
 FINISH_AT = 3
 SHIP_AT = 5
 LAND_AT = 7
@@ -184,25 +185,30 @@
     ends[-1] = SEG_ROWS + 1
     late = list(range(max(blocks - 2, 0), blocks))
     early = list(range(late[0]))
-    jobs = []
-    for j in early:
-        for step in range(SEG_ROWS + 1):
-            jobs.append((j, step))
-    marks = []
-    for k in range(GROUPS):
-        for j in late:
-            for step in range(ends[k - 1] if k else 0, ends[k]):
-                jobs.append((j, step))
+    lead = late[0] - 1
+    jobs = [(j, step) for j in early for step in range(SEG_ROWS + 1) if j != lead or step < ends[0]]
+    jobs += [(j, step) for j in late for step in range(ends[0])]
+    marks = [len(jobs)]
+    if early:
+        jobs += [(lead, step) for step in range(ends[0], SEG_ROWS + 1)]
+    for k in range(1, GROUPS):
+        jobs += [(j, step) for j in late for step in range(ends[k - 1], ends[k])]
         marks.append(len(jobs))
+    first = early[-1:] + late
+    old = early[:-1]
 
     def deliver(k):
         if k == 0:
             pl.semaphore_wait(barrier, devices - 1)
             ship(0, 0, blocks)
-            for group in range(1, GROUPS):
-                ship(group, 0, len(early))
-        elif k < GROUPS - 2:
-            ship(k, late[0], len(late))
+            if old:
+                for group in range(1, GROUPS):
+                    ship(group, 0, len(old))
+        elif k == 1:
+            ship(1, first[0], len(first))
+            if early:
+                for group in range(2, GROUPS):
+                    ship(group, lead, 1)
         elif k == GROUPS - 2:
             ship(k, late[0], len(late))
             ship(k + 1, late[0], len(late) - 1)
@@ -221,13 +227,16 @@
 
     plan(LAND_AT, land)
     for j in range(2, blocks):
-        plan((SEG_ROWS + 1) * (j - 2) + SEG_ROWS, functools.partial(prepare, j))
+        plan(SEG_ROWS + ends[0] * (j - 2), functools.partial(prepare, j))
+    if old:
+        plan(SEG_ROWS + 4, functools.partial(finish, 0, GROUPS, old))
+    plan(marks[0] + FINISH_AT, functools.partial(finish, 0, 1, first))
+    plan(marks[0] + SHIP_AT, functools.partial(deliver, 0))
     if early:
-        plan(marks[0] - 2, functools.partial(finish, 0, GROUPS, early))
-    for k in range(GROUPS - 1):
-        plan(marks[k] + FINISH_AT, functools.partial(finish, k, 1, late))
-        if k < GROUPS - 2:
-            plan(marks[k] + SHIP_AT, functools.partial(deliver, k))
+        plan(marks[1] - 3, functools.partial(finish, 1, GROUPS - 1, early[-1:]))
+    plan(marks[1] + FINISH_AT, functools.partial(finish, 1, 1, late))
+    plan(marks[1] + SHIP_AT, functools.partial(deliver, 1))
+    plan(marks[2] + FINISH_AT - 1, functools.partial(finish, 2, 1, late))
     plan(len(jobs) - 3, functools.partial(finish, GROUPS - 1, 1, late[:-1]))
     plan(len(jobs) - 1, functools.partial(deliver, GROUPS - 2))
     for n, (j, step) in enumerate(jobs):
@@ -255,7 +264,7 @@
 
 def map_kernel(
     span, total, got, guard_ref, size_ref, dft, tab, ker,
-    out_ref, power_ref, coef_ref,
+    out_hbm, out_ref, power_ref, coef_ref, out_sem,
 ):
     me = lax.axis_index("tm")
     rows_sent = window_rows(span)
@@ -323,7 +332,16 @@
     sums = sums[:, : 2 * total] + sums[:, 2 * total :] + coef_c * kernel
     high, low = split(sums)
     noise = mm(jnp.concatenate([high, low, high], 1), tab[...]) * weight
-    out_ref[...] = (power_c - floor_c) / (0.25 + noise)
+    copies = []
+    rows = span // PIECES
+    for p in range(PIECES):
+        piece = slice(p * rows, (p + 1) * rows)
+        out_ref[piece] = (power_c[piece] - floor_c[piece]) / (0.25 + noise[piece])
+        at = pl.ds(p * rows, rows)
+        copies.append(pltpu.make_async_copy(out_ref.at[at], out_hbm.at[at], out_sem.at[p]))
+        copies[-1].start()
+    for copy in copies:
+        copy.wait()
 
 
 def np_split(x):
@@ -387,10 +405,12 @@
         functools.partial(map_kernel, span, total),
         out_shape=jax.ShapeDtypeStruct((span, DOP), F32),
         in_specs=[vmem] * 6,
-        out_specs=vmem,
+        out_specs=hbm,
         scratch_shapes=[
+            pltpu.VMEM((span, DOP), F32),
             pltpu.VMEM((width, DOP + LANES), F32),
             pltpu.VMEM((width, 2 * total), F32),
+            pltpu.SemaphoreType.DMA((PIECES,)),
         ],
         compiler_params=pltpu.CompilerParams(vmem_limit_bytes=MAP_LIMIT),
         name="map",

time: 21.5 us -> 21.2 us (0.986)
  the two profiles are of different devices: /device:TPU:0 before, /device:TPU:16 now
where the time goes in v3:
time: 21.2 us; the launch traced here: 21.1 us
  Pallas kernels  19.7 us (93%)
  local copies, waits for them, and re-layouts  1.33 us (6%)
    pallas_call x1, Pallas kernels, body(): pl.pallas_call(functools.partial(correlate_kernel, span), out_shape=jax.S...  17.4 us
    pallas_call x1, Pallas kernels, body(): pl.pallas_call(functools.partial(map_kernel, span, total), out_shape=jax....  2.33 us
    unnamed x14, local copies, waits for them, and re-layouts  1.33 us

profile of v3, /device:TPU:16, one launch (start us, length us, event | category | flops | bytes accessed | tf_op | source)
XLA Modules:
  0.0 21.1 jit_solution(10691290973340794677)
XLA Ops:
  0.0 0.0 copy-start.5
  0.0 0.7 %copy-done.5 = s32[4]{0:T(128)S(1)} copy-done((s32[4]{0:T(128)S(1)}, s32[4]{0:T(128)}, u32[]{:S(2)}) %copy-start.5) | copy-done | bytes 40
  0.7 0.0 copy-start.6
  0.7 0.7 %copy-done.6 = s32[4]{0:T(128)S(1)} copy-done((s32[4]{0:T(128)S(1)}, s32[4]{0:T(128)}, u32[]{:S(2)}) %copy-start.6) | copy-done | bytes 40
  1.3 0.0 copy-start
  1.3 0.0 copy-start.1
  1.3 0.0 copy-start.2
  1.3 0.0 copy-start.3
  1.3 0.0 copy-start.4
  1.3 17.4 %correlate.1.got = f32[256,128]{1,0:T(8,128)S(1)} custom-call(s32[4]{0:T(128)S(1)} %copy-done.5, s32[4]{0:T(128)S(1)} %copy-done.6, bf16[4,1024,256]{2,1,0:T(8,128)(2,1)} %s_hbm.1, bf16[4,1040,256]{2,1,0:T(8,128)(2,1)} %e_hbm.1), custom_call_target="tpu_custom_call" | custom-call | tf_op jit(solution)/shard_map/correlate/pallas_call | solution.py:376
  18.7 0.0 copy-done
  18.7 0.0 copy-done.1
  18.7 0.0 copy-done.2
  18.7 0.0 copy-done.3
  18.7 0.0 copy-done.4
  18.7 2.3 %map.1 = f32[256,512]{1,0:T(8,128)} custom-call(f32[256,128]{1,0:T(8,128)S(1)} %correlate.1.got, s32[1,256]{1,0:T(1,128)S(1)} %bitcast.2, s32[1,256]{1,0:T(1,128)S(1)} %bitcast.3, bf16[512,128]{1,0:T(8,128)(2,1)S(1)} %copy-done.1, bf16[192,512]{1,0:T(8,128)(2,1)S(1)} %copy-done, bf16[128,128]{1,0:T(8,128)(2,1)S(1)} %copy-done.2), custom_call_target="tpu_custom_call" | custom-call | tf_op jit(solution)/shard_map/map/pallas_call | solution.py:404
Async XLA Ops:
  0.0 0.7 %copy-start.5 = (s32[4]{0:T(128)S(1)}, s32[4]{0:T(128)}, u32[]{:S(2)}) copy-start(s32[4]{0:T(128)} %walk_hbm.1) | copy-start | bytes 52
  0.7 0.7 %copy-start.6 = (s32[4]{0:T(128)S(1)}, s32[4]{0:T(128)}, u32[]{:S(2)}) copy-start(s32[4]{0:T(128)} %ids_hbm.1) | copy-start | bytes 52
  1.3 17.4 %copy-start = (bf16[192,512]{1,0:T(8,128)(2,1)S(1)}, bf16[192,512]{1,0:T(8,128)(2,1)}, u32[]{:S(2)}) copy-start(bf16[192,512]{1,0:T(8,128)(2,1)} %constant.7.clone.tab) | copy-start | bytes 589828
  1.3 17.4 %copy-start.1 = (bf16[512,128]{1,0:T(8,128)(2,1)S(1)}, bf16[512,128]{1,0:T(8,128)(2,1)}, u32[]{:S(2)}) copy-start(bf16[512,128]{1,0:T(8,128)(2,1)} %constant.6.clone.dft) | copy-start | bytes 393220
  1.3 17.4 %copy-start.2 = (bf16[128,128]{1,0:T(8,128)(2,1)S(1)}, bf16[128,128]{1,0:T(8,128)(2,1)}, u32[]{:S(2)}) copy-start(bf16[128,128]{1,0:T(8,128)(2,1)} %constant.8.clone.ker) | copy-start | bytes 98308
  1.3 17.4 %copy-start.3 = (s32[256]{0:T(256)S(1)}, s32[256]{0:T(256)}, u32[]{:S(2)}) copy-start(s32[256]{0:T(256)} %param.13) | copy-start | bytes 3076
  1.3 17.4 %copy-start.4 = (s32[256]{0:T(256)S(1)}, s32[256]{0:T(256)}, u32[]{:S(2)}) copy-start(s32[256]{0:T(256)} %param.14) | copy-start | bytes 3076

commit v4 on v3

--- a/solution.py
+++ b/solution.py
@@ -12,6 +12,7 @@
 D = 2048
 DOP = 512
 SEGS = 64
+WALK = 64
 GUARD_MAX = 8
 WIN_MAX = 16
 REACH = GUARD_MAX + WIN_MAX
@@ -49,8 +50,8 @@
 
 
 def correlate_kernel(
-    span, walk_hbm, ids_hbm, s_hbm, e_hbm, out_ref,
-    walk_ref, ids_ref, s_ref, e_ref, lhs_ref, rhs_ref, hold_ref, diag_ref, send, got,
+    span, code_hbm, s_hbm, e_hbm, out_ref,
+    code_ref, s_ref, e_ref, lhs_ref, rhs_ref, hold_ref, diag_ref, send, got,
     small_sem, piece_sem, in_sem, send_sem, recv_sem,
 ):
     blocks, rows_all = s_hbm.shape[:2]
@@ -62,10 +63,7 @@
     me = lax.axis_index("tm")
     barrier = pltpu.get_barrier_semaphore()
     peers = [lax.rem(me + k, devices) for k in range(1, devices)]
-    small = [
-        pltpu.make_async_copy(walk_hbm, walk_ref, small_sem.at[0]),
-        pltpu.make_async_copy(ids_hbm, ids_ref, small_sem.at[1]),
-    ]
+    small = [pltpu.make_async_copy(code_hbm, code_ref, small_sem.at[0])]
     loads = [
         [
             pltpu.make_async_copy(s_hbm.at[j], s_ref.at[j], in_sem.at[j, 0]),
@@ -147,8 +145,8 @@
         late_by = (LANES - iota((lines, LANES), 1)) & (LANES - 1)
         place = (iota((lines, LANES), 0) + base) * LANES + late_by
         for j in chosen:
-            shift = walk_ref[j] + REACH
-            label = jnp.full((1, LANES), ids_ref[j], jnp.int32).astype(F32)
+            shift = (code_ref[j] & (WALK - 1)) + REACH
+            label = jnp.full((1, LANES), code_ref[j] >> (WALK.bit_length() - 1), jnp.int32).astype(F32)
             for part in range(2):
                 y = diag_ref[j, part, pl.ds(base * 8, lines, stride=8), :]
                 y = pltpu.roll(y, LANES - shift, 1)
@@ -376,10 +374,9 @@
     windows = pl.pallas_call(
         functools.partial(correlate_kernel, span),
         out_shape=jax.ShapeDtypeStruct((total * pad, LANES), F32),
-        in_specs=[hbm] * 4,
+        in_specs=[hbm] * 3,
         out_specs=vmem,
         scratch_shapes=[
-            pltpu.SMEM((blocks,), jnp.int32),
             pltpu.SMEM((blocks,), jnp.int32),
             pltpu.VMEM(surveillance.shape, BF16),
             pltpu.VMEM(ref_samples.shape, BF16),
@@ -389,7 +386,7 @@
             pltpu.VMEM((blocks, 2, LINES * 8, LANES), F32),
             pltpu.VMEM(send_shape, F32),
             pltpu.VMEM(send_shape, F32),
-            pltpu.SemaphoreType.DMA((2,)),
+            pltpu.SemaphoreType.DMA((1,)),
             pltpu.SemaphoreType.DMA((rows_all // CHUNK, 2)),
             pltpu.SemaphoreType.DMA((blocks, 2)),
             pltpu.SemaphoreType.DMA((devices,)),
@@ -399,7 +396,7 @@
             collective_id=0, has_side_effects=True, vmem_limit_bytes=VMEM_LIMIT
         ),
         name="correlate",
-    )(walk, block_ids, surveillance, ref_samples)
+    )(block_ids * WALK + walk, surveillance, ref_samples)
     width = span + 2 * REACH if span % LANES == 0 else rows_sent * LANES
     return pl.pallas_call(
         functools.partial(map_kernel, span, total),

time: 21.2 us -> 20.6 us (0.972)
  local copies, waits for them, and re-layouts: 1.33 us -> 0.02 us
  other arithmetic: 0 us -> 0.67 us
    unnamed x14 -> x10, local copies, waits for them, and re-layouts: 1.33 us -> 0.02 us
    add x0 -> x1, other arithmetic: none -> 0.67 us  [body(): block_ids * WALK + walk]
where the time goes in v4:
time: 20.6 us; the launch traced here: 20.4 us
  Pallas kernels  19.7 us (96%)
  other arithmetic  0.67 us (3%)
    pallas_call x1, Pallas kernels, body(): pl.pallas_call(functools.partial(correlate_kernel, span), out_shape=jax.S...  17.4 us
    pallas_call x1, Pallas kernels, body(): pl.pallas_call(functools.partial(map_kernel, span, total), out_shape=jax....  2.32 us
    add x1, other arithmetic, body(): block_ids * WALK + walk  0.67 us

profile of v4, /device:TPU:16, one launch (start us, length us, event | category | flops | bytes accessed | tf_op | source)
XLA Modules:
  0.0 20.4 jit_solution(5458276456632830335)
XLA Ops:
  0.0 0.7 %multiply_add_fusion.code_hbm = s32[4]{0:T(128)S(1)} fusion(s32[4]{0:T(128)} %param.12, s32[4]{0:T(128)} %param.11), kind=kLoop, calls=%fused_computation | loop fusion | flops 8 | bytes 48 | tf_op jit(solution)/shard_map/add | solution.py:399
  0.7 0.0 copy-start
  0.7 0.0 copy-start.1
  0.7 0.0 copy-start.2
  0.7 0.0 copy-start.3
  0.7 0.0 copy-start.4
  0.7 17.4 %correlate.1.got = f32[256,128]{1,0:T(8,128)S(1)} custom-call(s32[4]{0:T(128)S(1)} %multiply_add_fusion.code_hbm, bf16[4,1024,256]{2,1,0:T(8,128)(2,1)} %s_hbm.1, bf16[4,1040,256]{2,1,0:T(8,128)(2,1)} %e_hbm.1), custom_call_target="tpu_custom_call" | custom-call | tf_op jit(solution)/shard_map/correlate/pallas_call | solution.py:374
  18.1 0.0 copy-done
  18.1 0.0 copy-done.1
  18.1 0.0 copy-done.2
  18.1 0.0 copy-done.3
  18.1 0.0 copy-done.4
  18.1 2.3 %map.1 = f32[256,512]{1,0:T(8,128)} custom-call(f32[256,128]{1,0:T(8,128)S(1)} %correlate.1.got, s32[1,256]{1,0:T(1,128)S(1)} %bitcast.2, s32[1,256]{1,0:T(1,128)S(1)} %bitcast.3, bf16[512,128]{1,0:T(8,128)(2,1)S(1)} %copy-done.1, bf16[192,512]{1,0:T(8,128)(2,1)S(1)} %copy-done, bf16[128,128]{1,0:T(8,128)(2,1)S(1)} %copy-done.2), custom_call_target="tpu_custom_call" | custom-call | tf_op jit(solution)/shard_map/map/pallas_call | solution.py:401
Async XLA Ops:
  0.7 17.4 %copy-start = (bf16[192,512]{1,0:T(8,128)(2,1)S(1)}, bf16[192,512]{1,0:T(8,128)(2,1)}, u32[]{:S(2)}) copy-start(bf16[192,512]{1,0:T(8,128)(2,1)} %constant.9.clone.tab) | copy-start | bytes 589828
  0.7 17.4 %copy-start.1 = (bf16[512,128]{1,0:T(8,128)(2,1)S(1)}, bf16[512,128]{1,0:T(8,128)(2,1)}, u32[]{:S(2)}) copy-start(bf16[512,128]{1,0:T(8,128)(2,1)} %constant.8.clone.dft) | copy-start | bytes 393220
  0.7 17.4 %copy-start.2 = (bf16[128,128]{1,0:T(8,128)(2,1)S(1)}, bf16[128,128]{1,0:T(8,128)(2,1)}, u32[]{:S(2)}) copy-start(bf16[128,128]{1,0:T(8,128)(2,1)} %constant.10.clone.ker) | copy-start | bytes 98308
  0.7 17.4 %copy-start.3 = (s32[256]{0:T(256)S(1)}, s32[256]{0:T(256)}, u32[]{:S(2)}) copy-start(s32[256]{0:T(256)} %param.13) | copy-start | bytes 3076
  0.7 17.4 %copy-start.4 = (s32[256]{0:T(256)S(1)}, s32[256]{0:T(256)}, u32[]{:S(2)}) copy-start(s32[256]{0:T(256)} %param.14) | copy-start | bytes 3076
